TPU v7x, 32 devices: a whole 2x2x4 slice. The times are simulated.
32 devices in a mesh: vocab: 32 (over z, y, x, core).
Axes of the slice: x: 2, y: 2, z: 4, core: 2. Of those that a mesh axis runs over, the one named last changes fastest.
Arguments:
- hidden: bfloat16 [2, 256, 3584], P(None, 'vocab'), may hold values from -256 to 256
- head_weight: bfloat16 [3584, 24576], P(None, 'vocab'), may hold values from -1 to 1
- teacher: bfloat16 [2, 256, 24576], P(None, None, 'vocab'), may hold values from 0 to 1
Outputs:
- token_loss: float32 [2, 256], P(None, 'vocab')
- hidden_grad: bfloat16 [2, 256, 3584], P(None, 'vocab')
- head_grad: bfloat16 [3584, 24576], P(None, 'vocab')
All inputs are finite; a program needn't handle non-finite values.
Results may differ from a plain program's by a relative error of at most 0.012.
Values may be sent and summed in bfloat16 or wider, within the bound.
A program may use at most 128 MiB of HBM per device.

v0:
```python
import jax
import jax.numpy as jnp
from jax import lax
from jax.sharding import PartitionSpec as P


def finish(logit_block, target_block):
    target_wide = target_block.astype(jnp.float32)
    teacher_mass = jnp.sum(target_wide, axis=-1)
    cross_term = jnp.sum(target_wide * logit_block, axis=-1)
    peak_logit = jnp.max(logit_block, axis=-1)
    peak_logit = lax.pmax(peak_logit, "vocab")
    exp_total = jnp.sum(jnp.exp(logit_block - peak_logit[..., None]), axis=-1)
    exp_total, teacher_mass, cross_term = lax.psum((exp_total, teacher_mass, cross_term), "vocab")
    log_norm = peak_logit + jnp.log(exp_total)
    token_loss = teacher_mass * log_norm - cross_term
    logit_grad = (
        teacher_mass[..., None] * jnp.exp(logit_block - log_norm[..., None]) - target_wide
    ).astype(jnp.bfloat16)
    return (token_loss, logit_grad)


def shards(hidden, head_weight, teacher):
    group_count, row_count, model_width = hidden.shape
    contract = (((1,), (1,)), ((), ()))
    shard_rows = lax.all_gather(hidden, "vocab", axis=1, tiled=True)
    logits = jnp.einsum("crd,dv->crv", shard_rows, head_weight, preferred_element_type=jnp.float32)
    token_loss, logit_grad = finish(logits, teacher)
    row_total = lax.axis_size("vocab") * (group_count * row_count)
    per_group = row_total // group_count
    owner_count = per_group // row_count
    grad_block = logit_grad
    grad_block = (
        grad_block.reshape(group_count, owner_count, row_count, -1)
        .transpose(1, 0, 2, 3)
        .reshape(row_total, -1)
    )
    summed = lax.psum_scatter(
        lax.dot_general(grad_block, head_weight, contract, preferred_element_type=jnp.float32),
        "vocab",
        scatter_dimension=0,
        tiled=True,
    )
    hidden_grad = summed.reshape(group_count, row_count, model_width).astype(jnp.bfloat16)
    weight_grad = jnp.zeros((model_width, head_weight.shape[1]), jnp.bfloat16)
    for group_index in range(group_count):
        product_term = lax.dot_general(
            shard_rows[group_index],
            logit_grad[group_index],
            (((0,), (0,)), ((), ())),
            preferred_element_type=jnp.float32,
        )
        weight_grad = (weight_grad.astype(jnp.float32) + product_term).astype(jnp.bfloat16)
    own_loss = lax.dynamic_slice_in_dim(
        token_loss, lax.axis_index("vocab") * row_count, row_count, 1
    )
    return (own_loss, hidden_grad, weight_grad)


def solution(mesh):
    in_specs = (P(None, "vocab", None), P(None, "vocab"), P(None, None, "vocab"))
    out_specs = (P(None, "vocab"), P(None, "vocab", None), P(None, "vocab"))
    return jax.shard_map(shards, mesh=mesh, in_specs=in_specs, out_specs=out_specs, check_vma=False)
```

profile of v0, /device:TPU:0, one launch (start us, length us, event | category | flops | bytes accessed | tf_op | source)
XLA Modules:
  0.0 325.6 jit_solution(7871215503381196824)
XLA Ops:
  7.2 0.0 all-gather.2.cloned.1.call-start
  7.2 0.7 all-gather.2.cloned.1.call-update
  7.9 0.0 copy-start.1
  7.9 0.0 reduce-scatter.2.cloned.1.call-start
  8.0 66.4 %all-gather.2.cloned.1.call-done = bf16[2,256,3584]{2,1,0:T(8,128)(2,1)} async-done(((bf16[2,8,3584]{2,1,0:T(8,128)(2,1)}), bf16[2,256,3584]{2,1,0:T(8,128)(2,1)}) %all-gather.2.cloned.1.call-update) | async-done | bytes 3670032 | tf_op jit(solution)/shard_map/all_gather | solution.py:26
  74.3 6.8 %fusion.5 = (f32[2,256]{1,0:T(2,128)S(1)}, f32[2,256,768]{2,1,0:T(8,128)S(1)}) fusion(bf16[2,256,3584]{2,1,0:T(8,128)(2,1)} %all-gather.2.cloned.1.call-done, bf16[3584,768]{1,0:T(8,128)(2,1)} %param.4), kind=kOutput, calls=%fused_computation.19 | convolution fusion | flops 2818964992 | bytes 10749952 | tf_op jit(solution)/shard_map/crd,dv->crv/dot_general | solution.py:27
  81.1 38.5 %pmax.7 = f32[2,256]{1,0:T(2,128)S(1)} all-reduce(f32[2,256]{1,0:T(2,128)S(1)} %get-tuple-element.15), channel_id=1, replica_groups=mesh['vocab'=32] {'vocab'}, use_global_device_ids=true, to_apply=%region_3.0 | all-reduce | flops 512 | bytes 4096 | tf_op jit(solution)/shard_map/pmax | solution.py:12
  119.6 0.0 copy-done.1
  119.6 0.7 exponential_reduce_fusion
  120.4 40.7 %all-reduce = (f32[2,256]{1,0:T(2,128)S(1)}, f32[2,256]{1,0:T(2,128)S(1)}, f32[2,256]{1,0:T(2,128)S(1)}) all-reduce(f32[2,256]{1,0:T(2,128)S(1)} %get-tuple-element.10, f32[2,256]{1,0:T(2,128)S(1)} %get-tuple-element.9, f32[2,256]{1,0:T(2,128)S(1)} %get-tuple-element.11), channel_id=1, replica_groups=mesh['vocab'=32] {'vocab'}, use_global_device_ids=true, to_apply=%region_7.0 | all-reduce | flops 1536 | bytes 12288 | tf_op jit(solution)/shard_map/psum | solution.py:14
  161.0 0.4 fusion.4
  161.5 0.1 copy.7
  161.5 7.7 %fusion.6 = f32[512,3584]{1,0:T(8,128)} fusion(bf16[512,768]{1,0:T(8,128)(2,1)S(1)} %bitcast.29, bf16[3584,768]{1,0:T(8,128)(2,1)} %param.4), kind=kOutput, calls=%fused_computation.20 | convolution fusion | flops 2818572288 | bytes 13631488 | tf_op jit(solution)/shard_map/dot_general | solution.py:39
  169.2 0.0 reduce-scatter.2.cloned.1.call-update
  169.3 0.0 copy-start
  169.3 3.3 %convolution_convert_fusion = bf16[768,3584]{1,0:T(8,128)(2,1)S(1)} fusion(bf16[2,256,3584]{2,1,0:T(8,128)(2,1)} %all-gather.2.cloned.1.call-done, bf16[2,256,768]{2,1,0:T(8,128)(2,1)S(1)} %fusion.4), kind=kOutput, calls=%fused_computation.1 | convolution fusion | flops 1412038656 | bytes 7733248 | tf_op jit(solution)/shard_map/dot_general | solution.py:47
  172.6 0.0 copy-done
  172.6 4.0 %fusion = bf16[3584,768]{0,1:T(8,128)(2,1)} fusion(bf16[768,3584]{1,0:T(8,128)(2,1)S(1)} %convolution_convert_fusion, bf16[2,256,3584]{2,1,0:T(8,128)(2,1)S(1)} %copy-done, bf16[2,256,768]{2,1,0:T(8,128)(2,1)S(1)} %fusion.4), kind=kOutput, calls=%fused_computation.2 | convolution fusion | flops 1417543680 | bytes 13238272 | tf_op jit(solution)/shard_map/dot_general | solution.py:47
  176.6 8.3 %copy.8 = bf16[3584,768]{1,0:T(8,128)(2,1)} copy(bf16[3584,768]{0,1:T(8,128)(2,1)} %fusion) | data formatting | bytes 11010048
  184.9 0.6 dynamic-slice_subtract_fusion
  185.5 131.7 %reduce-scatter.2.cloned.1.call-done = f32[16,3584]{1,0:T(8,128)} async-done(((f32[512,3584]{1,0:T(8,128)}), f32[16,3584]{1,0:T(8,128)}) %reduce-scatter.2.cloned.1.call-update) | async-done | bytes 229392 | tf_op jit(solution)/shard_map/reduce_scatter | solution.py:38
  317.2 1.6 convert_bitcast_fusion
  (1 shorter events, 0.0 us)
Async XLA Ops:
  7.2 67.2 %all-gather.2.cloned.1.call-start = ((), (), s32[]{:S(2)}) async-start(), calls=%async_computation.1 | async-start | bytes 3784704 | tf_op jit(solution)/shard_map/all_gather | solution.py:26
  7.9 111.7 %copy-start.1 = (bf16[2,256,768]{2,1,0:T(8,128)(2,1)S(1)}, bf16[2,256,768]{2,1,0:T(8,128)(2,1)}, u32[]{:S(2)}) copy-start(bf16[2,256,768]{2,1,0:T(8,128)(2,1)} %param.5) | copy-start | bytes 2359300
  7.9 309.3 %reduce-scatter.2.cloned.1.call-start = ((), (), s32[]{:S(2)}) async-start(), calls=%async_computation.2 | async-start | bytes 7569408 | tf_op jit(solution)/shard_map/reduce_scatter | solution.py:38
  169.3 3.3 %copy-start = (bf16[2,256,3584]{2,1,0:T(8,128)(2,1)S(1)}, bf16[2,256,3584]{2,1,0:T(8,128)(2,1)}, u32[]{:S(2)}) copy-start(bf16[2,256,3584]{2,1,0:T(8,128)(2,1)} %all-gather.2.cloned.1.call-done) | copy-start | bytes 11010052
Sparse Core Ops, SparseCore 0:
  10.9 63.4 all-gather.1
  169.4 147.7 reduce-scatter.1
where the time goes:
time: 326 us
  waiting for transfers between devices  199 us (61%)
  blocking collectives  79.2 us (24%)
  matrix products  21.8 us (7%)
  between operations  14.1 us (4%)
  local copies, waits for them, and re-layouts  8.33 us (3%)
  other arithmetic  3.38 us (1%)
    reduce_scatter x1, waiting for transfers between devices, shards(): lax.psum_scatter(lax.dot_general(grad_block, head_weight, contract, prefe...  132 us
    all_gather x1, waiting for transfers between devices, shards(): shard_rows = lax.all_gather(hidden, 'vocab', axis=1, tiled=True)  66.4 us
    psum x1, blocking collectives, finish(): lax.psum((exp_total, teacher_mass, cross_term), 'vocab')  40.7 us
    pmax x1, blocking collectives, finish(): peak_logit = lax.pmax(peak_logit, 'vocab')  38.5 us
    unnamed x5, local copies, waits for them, and re-layouts  8.28 us
    dot_general x1, matrix products, shards(): lax.dot_general(grad_block, head_weight, contract, preferred_element_type...  7.71 us
    dot_general x2, matrix products, shards(): lax.dot_general(shard_rows[group_index], logit_grad[group_index], (((0,),...  7.29 us
    dot_general x1, matrix products, shards(): jnp.einsum('crd,dv->crv', shard_rows, head_weight, preferred_element_type...  6.76 us
  transfers between devices with their start and end apart: 2, of which 2 were waited for; matrix products, arithmetic and copies ran while one was open for 5% of the time, Pallas kernels for 0%

commit v1 on v0

--- a/solution.py
+++ b/solution.py
@@ -1,7 +1,12 @@
 import jax
 import jax.numpy as jnp
 from jax import lax
+from jax.experimental import pallas as pl
+from jax.experimental.pallas import tpu as pltpu
 from jax.sharding import PartitionSpec as P
+import functools
+
+MESH = pl.DeviceIdType.MESH
 
 
 def finish(logit_block, target_block):
@@ -20,7 +25,7 @@
     return (token_loss, logit_grad)
 
 
-def shards(hidden, head_weight, teacher):
+def plain_shards(hidden, head_weight, teacher):
     group_count, row_count, model_width = hidden.shape
     contract = (((1,), (1,)), ((), ()))
     shard_rows = lax.all_gather(hidden, "vocab", axis=1, tiled=True)
@@ -57,7 +62,269 @@
     return (own_loss, hidden_grad, weight_grad)
 
 
+def subsets(bits):
+    masks = [0]
+    for b in bits:
+        masks += [m | (1 << b) for m in masks]
+    return masks
+
+
+def axis_orders(bit_count):
+    axes = [[b] for b in range(1, min(bit_count, 3))] + [list(range(bit_count - 1, 2, -1))]
+    x, y, z = axes
+    return [z + y + x + [0], y + x + z + [0], x + z + y + [0]]
+
+
+def kernel(n, parts, hid, w_hbm, t_hbm, hfull, dl_hbm, hgrad, loss,
+           hbuf, w, t, logits, dl, g, rbuf, st, stc, wide,
+           ag_send, ag_recv, rs_send, rs_recv, st_send, st_recv, local):
+    bit_count = n.bit_length() - 1
+    me = lax.axis_index("vocab")
+    flip = [(1 - 2 * ((me // (1 << b)) % 2)) * (1 << b) for b in range(bit_count)]
+
+    def at(mask):
+        return me + sum(flip[b] for b in range(bit_count) if mask >> b & 1)
+
+    rows, width = hid.shape
+    tokens, columns = dl.shape
+    orders = axis_orders(bit_count)
+    part_ids = range(len(parts))
+
+    copy_w = [
+        pltpu.make_async_copy(w_hbm.at[pl.ds(o, c)], w.at[pl.ds(o, c)], local.at[i])
+        for i, (o, c) in enumerate(parts)
+    ]
+    copy_t = pltpu.make_async_copy(t_hbm, t, local.at[3])
+    copy_own = pltpu.make_async_copy(hid, hbuf.at[me], local.at[4])
+    copy_own.start()
+
+    barrier = pltpu.get_barrier_semaphore()
+    for b in range(bit_count):
+        pl.semaphore_signal(barrier, inc=1, device_id=(at(1 << b),), device_id_type=MESH)
+    pl.semaphore_wait(barrier, bit_count)
+    copy_own.wait()
+
+    def gather_copy(p, b, r):
+        o, c = parts[p]
+        block = hbuf.at[at(r), :, pl.ds(o, c)]
+        k = r | (1 << b)
+        return pltpu.make_async_remote_copy(
+            src_ref=block, dst_ref=block,
+            send_sem=ag_send.at[p, k], recv_sem=ag_recv.at[p, k],
+            device_id=(at(1 << b),), device_id_type=MESH)
+
+    def gather_arrival(p, b, r):
+        o, c = parts[p]
+        block = hbuf.at[at(r | (1 << b)), :, pl.ds(o, c)]
+        k = r | (1 << b)
+        return pltpu.make_async_remote_copy(
+            src_ref=block, dst_ref=block,
+            send_sem=ag_send.at[p, k], recv_sem=ag_recv.at[p, k],
+            device_id=(at(1 << b),), device_id_type=MESH)
+
+    def logits_part(p):
+        o, c = parts[p]
+        copy_w[p].wait()
+
+        @pl.loop(0, columns // 256)
+        def _(j):
+            cols = pl.ds(pl.multiple_of(j * 256, 256), 256)
+            term = jnp.dot(hbuf[:, :, o:o + c].reshape(tokens, c), w[o:o + c, cols],
+                           preferred_element_type=jnp.float32)
+            if p == 0:
+                logits[:, cols] = term
+            else:
+                logits[:, cols] += term
+
+    for s in range(bit_count):
+        for p in part_ids:
+            b = orders[p][s]
+            if s:
+                prev = orders[p][s - 1]
+                for r in subsets(orders[p][:s - 1]):
+                    gather_arrival(p, prev, r).wait_recv()
+            for r in subsets(orders[p][:s]):
+                gather_copy(p, b, r).start()
+        if s == 0:
+            for p in part_ids:
+                copy_w[p].start()
+            copy_t.start()
+    for p in part_ids:
+        for r in subsets(orders[p][:-1]):
+            gather_arrival(p, orders[p][-1], r).wait_recv()
+        logits_part(p)
+    for p in part_ids:
+        for s in range(bit_count):
+            for r in subsets(orders[p][:s]):
+                gather_copy(p, orders[p][s], r).wait_send()
+    out_h = pltpu.make_async_copy(hbuf, hfull, local.at[5])
+    out_h.start()
+    copy_t.wait()
+
+    chunk = 64
+
+    @pl.loop(0, tokens // chunk)
+    def _(i):
+        ds = pl.ds(pl.multiple_of(i * chunk, chunk), chunk)
+        l = logits[ds, :]
+        tw = t[ds, :].astype(jnp.float32)
+        peak = jnp.max(l, axis=-1, keepdims=True)
+        total = jnp.sum(jnp.exp(l - peak), axis=-1, keepdims=True)
+        mass = jnp.sum(tw, axis=-1, keepdims=True)
+        cross = jnp.sum(tw * l, axis=-1, keepdims=True)
+        lane = lax.broadcasted_iota(jnp.int32, (chunk, 128), 1)
+        st[ds, :] = jnp.where(lane == 0, peak, jnp.where(lane == 1, total, jnp.where(lane == 2, mass, cross)))
+
+    stc[0] = st[...].T[0:8]
+    for b in range(bit_count):
+        copy = pltpu.make_async_remote_copy(
+            src_ref=stc.at[2 * b], dst_ref=stc.at[2 * b + 1],
+            send_sem=st_send.at[b], recv_sem=st_recv.at[b],
+            device_id=(at(1 << b),), device_id_type=MESH)
+        copy.start()
+        copy.wait()
+        mine, other = stc[2 * b], stc[2 * b + 1]
+        peak = jnp.maximum(mine[0:1], other[0:1])
+        total = mine[1:2] * jnp.exp(mine[0:1] - peak) + other[1:2] * jnp.exp(other[0:1] - peak)
+        sums = mine + other
+        row = lax.broadcasted_iota(jnp.int32, sums.shape, 0)
+        stc[2 * b + 2] = jnp.where(row == 0, peak, jnp.where(row == 1, total, sums))
+    final = stc[2 * bit_count]
+    log_norm = final[0:1] + jnp.log(final[1:2])
+    mass = final[2:3]
+    loss[...] = jnp.broadcast_to(mass * log_norm - final[3:4], loss.shape)
+    row = lax.broadcasted_iota(jnp.int32, (8, tokens), 0)
+    wide[...] = jnp.zeros(wide.shape, jnp.float32)
+    wide[0:8] = jnp.where(row == 0, log_norm, mass)
+    st[...] = wide[...].T
+
+    @pl.loop(0, tokens // chunk)
+    def _(i):
+        ds = pl.ds(pl.multiple_of(i * chunk, chunk), chunk)
+        s = st[ds, :]
+        dl[ds, :] = (s[:, 1:2] * jnp.exp(logits[ds, :] - s[:, 0:1]) - t[ds, :].astype(jnp.float32)).astype(jnp.bfloat16)
+
+    out_dl = pltpu.make_async_copy(dl, dl_hbm, local.at[6])
+    out_dl.start()
+
+    def scatter_copy(p, s, r):
+        o, c = parts[p]
+        b = orders[p][bit_count - 1 - s]
+        k = r | (1 << b)
+        return pltpu.make_async_remote_copy(
+            src_ref=g.at[at(k), :, pl.ds(o, c)], dst_ref=rbuf.at[k, :, pl.ds(o, c)],
+            send_sem=rs_send.at[p, k], recv_sem=rs_recv.at[p, k],
+            device_id=(at(1 << b),), device_id_type=MESH)
+
+    def left(p, s):
+        return subsets(orders[p][:bit_count - 1 - s])
+
+    for p in part_ids:
+        o, c = parts[p]
+
+        @pl.loop(0, c // 256)
+        def _(j):
+            ds = pl.ds(pl.multiple_of(o + j * 256, 256), 256)
+            term = lax.dot_general(dl[...], w[ds, :], (((1,), (1,)), ((), ())),
+                                   preferred_element_type=jnp.float32)
+            g[:, :, ds] = term.astype(jnp.bfloat16).reshape(n, rows, 256)
+
+        for r in left(p, 0):
+            scatter_copy(p, 0, r).start()
+    for s in range(bit_count):
+        for p in part_ids:
+            o, c = parts[p]
+            b = orders[p][bit_count - 1 - s]
+            for r in left(p, s):
+                scatter_copy(p, s, r).wait_recv()
+                k = r | (1 << b)
+                total = g[at(r), :, o:o + c].astype(jnp.float32) + rbuf[k, :, o:o + c].astype(jnp.float32)
+                if s == bit_count - 1:
+                    hgrad[:, o:o + c] = total.astype(jnp.bfloat16)
+                else:
+                    g[at(r), :, o:o + c] = total.astype(jnp.bfloat16)
+            if s < bit_count - 1:
+                for r in left(p, s + 1):
+                    scatter_copy(p, s + 1, r).start()
+    for p in part_ids:
+        for s in range(bit_count):
+            for r in left(p, s):
+                scatter_copy(p, s, r).wait_send()
+    out_h.wait()
+    out_dl.wait()
+
+
+def split_width(width):
+    tiles = width // 256
+    third = -(-tiles // 3)
+    sizes = [third, tiles - 2 * third, third]
+    parts, at = [], 0
+    for size in sizes:
+        parts.append((at * 256, size * 256))
+        at += size
+    return parts
+
+
+def shards(n, hidden, head_weight, teacher):
+    group_count, row_count, width = hidden.shape
+    columns = head_weight.shape[1]
+    rows = group_count * row_count
+    tokens = n * rows
+    bf16, f32 = jnp.bfloat16, jnp.float32
+    bit_count = n.bit_length() - 1
+    parts = split_width(width)
+    by_owner = (
+        teacher.reshape(group_count, n, row_count, columns).transpose(1, 0, 2, 3).reshape(tokens, columns)
+    )
+    vmem = pl.BlockSpec(memory_space=pltpu.VMEM)
+    hbm = pl.BlockSpec(memory_space=pl.ANY)
+    dma = pltpu.SemaphoreType.DMA
+    hfull, dl, hgrad, loss = pl.pallas_call(
+        functools.partial(kernel, n, parts),
+        out_shape=[
+            jax.ShapeDtypeStruct((n, rows, width), bf16),
+            jax.ShapeDtypeStruct((tokens, columns), bf16),
+            jax.ShapeDtypeStruct((rows, width), bf16),
+            jax.ShapeDtypeStruct((8, tokens), f32),
+        ],
+        in_specs=[vmem, hbm, hbm],
+        out_specs=[hbm, hbm, vmem, vmem],
+        scratch_shapes=[
+            pltpu.VMEM((n, rows, width), bf16),
+            pltpu.VMEM((width, columns), bf16),
+            pltpu.VMEM((tokens, columns), bf16),
+            pltpu.VMEM((tokens, columns), f32),
+            pltpu.VMEM((tokens, columns), bf16),
+            pltpu.VMEM((n, rows, width), bf16),
+            pltpu.VMEM((n, rows, width), bf16),
+            pltpu.VMEM((tokens, 128), f32),
+            pltpu.VMEM((2 * bit_count + 1, 8, tokens), f32),
+            pltpu.VMEM((128, tokens), f32),
+            dma((3, n)), dma((3, n)), dma((3, n)), dma((3, n)),
+            dma((bit_count,)), dma((bit_count,)), dma((8,)),
+        ],
+        compiler_params=pltpu.CompilerParams(
+            collective_id=0, has_side_effects=True, vmem_limit_bytes=58 * 1024 * 1024),
+    )(hidden.reshape(rows, width), head_weight, by_owner)
+    weight_grad = lax.dot_general(
+        hfull.reshape(tokens, width), dl, (((0,), (0,)), ((), ())), preferred_element_type=f32
+    ).astype(bf16)
+    own_loss = lax.dynamic_slice_in_dim(loss[0], lax.axis_index("vocab") * rows, rows, 0)
+    return (own_loss.reshape(group_count, row_count), hgrad.reshape(group_count, row_count, width), weight_grad)
+
+
+def choose(n, hidden, head_weight, teacher):
+    group_count, row_count, width = hidden.shape
+    fits = (
+        n >= 16 and n & (n - 1) == 0 and group_count * row_count % 16 == 0
+        and width % 256 == 0 and width >= 1024 and head_weight.shape[1] % 256 == 0
+    )
+    if fits:
+        return shards(n, hidden, head_weight, teacher)
+    return plain_shards(hidden, head_weight, teacher)
+
+
 def solution(mesh):
     in_specs = (P(None, "vocab", None), P(None, "vocab"), P(None, None, "vocab"))
     out_specs = (P(None, "vocab"), P(None, "vocab", None), P(None, "vocab"))
-    return jax.shard_map(shards, mesh=mesh, in_specs=in_specs, out_specs=out_specs, check_vma=False)
+    return jax.shard_map(functools.partial(choose, mesh.shape["vocab"]), mesh=mesh, in_specs=in_specs, out_specs=out_specs, check_vma=False)

time: 326 us -> 96.7 us (0.30)
  waiting for transfers between devices: 199 us -> 0 us
  Pallas kernels: 0 us -> 83.9 us
  blocking collectives: 79.2 us -> 0 us
  matrix products: 21.8 us -> 7.77 us
  between operations: 14.1 us -> 0.65 us
  local copies, waits for them, and re-layouts: 8.33 us -> 4.17 us
  other arithmetic: 3.38 us -> 0 us
    reduce_scatter x1 -> x0, waiting for transfers between devices: 132 us -> none  [shards(): lax.psum_scatter(lax.dot_general(grad_block, head_weight, contract, prefe...]
    pallas_call x0 -> x1, Pallas kernels: none -> 83.9 us  [shards(): pl.pallas_call(functools.partial(kernel, n, parts), out_shape=[jax.ShapeD...]
    all_gather x1 -> x0, waiting for transfers between devices: 66.4 us -> none  [shards(): shard_rows = lax.all_gather(hidden, 'vocab', axis=1, tiled=True)]
    psum x1 -> x0, blocking collectives: 40.7 us -> none  [finish(): lax.psum((exp_total, teacher_mass, cross_term), 'vocab')]
    pmax x1 -> x0, blocking collectives: 38.5 us -> none  [finish(): peak_logit = lax.pmax(peak_logit, 'vocab')]
    dot_general x4 -> x1, matrix products: 21.8 us -> 7.77 us  [shards(): lax.dot_general(hfull.reshape(tokens, width), dl, (((0,), (0,)), ((), ())...]
    unnamed x5 -> x3, local copies, waits for them, and re-layouts: 8.28 us -> 0.65 us
  transfers between devices with their start and end apart: 2 -> 0, of which waited for: 2 -> 0; matrix products, arithmetic and copies ran while one was open for 5% -> 0% of each run, Pallas kernels for 0% -> 0%
where the time goes in v1:
time: 96.7 us; the launch traced here: 96.5 us
  Pallas kernels  83.9 us (87%)
  matrix products  7.77 us (8%)
  local copies, waits for them, and re-layouts  4.17 us (4%)
    pallas_call x1, Pallas kernels, shards(): pl.pallas_call(functools.partial(kernel, n, parts), out_shape=[jax.ShapeD...  83.9 us
    dot_general x1, matrix products, shards(): lax.dot_general(hfull.reshape(tokens, width), dl, (((0,), (0,)), ((), ())...  7.77 us
    reshape x1, local copies, waits for them, and re-layouts, shards(): teacher.reshape(group_count, n, row_count, columns).transpose(1, 0, 2, 3)  2.07 us

profile of v1, /device:TPU:0, one launch (start us, length us, event | category | flops | bytes accessed | tf_op | source)
XLA Modules:
  0.0 96.5 jit_solution(10620073007055704371)
XLA Ops:
  0.6 2.1 %copy.6 = bf16[2,32,8,768]{3,2,0,1:T(8,128)(2,1)} copy(bf16[2,32,8,768]{3,2,1,0:T(8,128)(2,1)} %bitcast.10) | data formatting | bytes 1572864 | tf_op jit(solution)/shard_map/reshape | solution.py:277
  2.7 83.9 %shard_map.58 = (bf16[32,16,3584]{2,1,0:T(8,128)(2,1)}, bf16[512,768]{1,0:T(8,128)(2,1)}, bf16[16,3584]{1,0:T(8,128)(2,1)}, f32[8,512]{1,0:T(8,128)}) custom-call(bf16[16,3584]{1,0:T(8,128)(2,1)} %bitcast.12, bf16[3584,768]{1,0:T(8,128)(2,1)} %w_hbm.1, bf16[512,768]{1,0:T(8,128)(2,1)} %bitcast.9), custom_call_target="tpu_custom_call" | custom-call | tf_op jit(solution)/shard_map/pallas_call | solution.py:282
  86.6 0.7 slice.3
  87.3 0.1 dynamic-slice_reduce_fusion
  87.4 0.6 reshape.29
  88.0 0.0 copy-start
  88.0 7.8 %convolution_convert_fusion = bf16[3584,768]{1,0:T(8,128)(2,1)} fusion(bf16[512,3584]{1,0:T(8,128)(2,1)} %bitcast.13, bf16[512,768]{1,0:T(8,128)(2,1)} %get-tuple-element.10), kind=kOutput, calls=%fused_computation | convolution fusion | flops 2821324800 | bytes 9961472 | tf_op jit(solution)/shard_map/dot_general | solution.py:309
  95.8 0.0 copy-done
  95.8 0.6 copy.8
Async XLA Ops:
  88.0 7.8 %copy-start = (bf16[16,3584]{1,0:T(8,128)(2,1)S(1)}, bf16[16,3584]{1,0:T(8,128)(2,1)}, u32[]{:S(2)}) copy-start(bf16[16,3584]{1,0:T(8,128)(2,1)} %get-tuple-element.8) | copy-start | bytes 344068

commit v2 on v1

v2 whole, which is shorter than its diff:
```python
import jax
import jax.numpy as jnp
from jax import lax
from jax.experimental import pallas as pl
from jax.experimental.pallas import tpu as pltpu
from jax.sharding import PartitionSpec as P
import functools

MESH = pl.DeviceIdType.MESH


def finish(logit_block, target_block):
    target_wide = target_block.astype(jnp.float32)
    teacher_mass = jnp.sum(target_wide, axis=-1)
    cross_term = jnp.sum(target_wide * logit_block, axis=-1)
    peak_logit = jnp.max(logit_block, axis=-1)
    peak_logit = lax.pmax(peak_logit, "vocab")
    exp_total = jnp.sum(jnp.exp(logit_block - peak_logit[..., None]), axis=-1)
    exp_total, teacher_mass, cross_term = lax.psum((exp_total, teacher_mass, cross_term), "vocab")
    log_norm = peak_logit + jnp.log(exp_total)
    token_loss = teacher_mass * log_norm - cross_term
    logit_grad = (
        teacher_mass[..., None] * jnp.exp(logit_block - log_norm[..., None]) - target_wide
    ).astype(jnp.bfloat16)
    return (token_loss, logit_grad)


def plain_shards(hidden, head_weight, teacher):
    group_count, row_count, model_width = hidden.shape
    contract = (((1,), (1,)), ((), ()))
    shard_rows = lax.all_gather(hidden, "vocab", axis=1, tiled=True)
    logits = jnp.einsum("crd,dv->crv", shard_rows, head_weight, preferred_element_type=jnp.float32)
    token_loss, logit_grad = finish(logits, teacher)
    row_total = lax.axis_size("vocab") * (group_count * row_count)
    per_group = row_total // group_count
    owner_count = per_group // row_count
    grad_block = logit_grad
    grad_block = (
        grad_block.reshape(group_count, owner_count, row_count, -1)
        .transpose(1, 0, 2, 3)
        .reshape(row_total, -1)
    )
    summed = lax.psum_scatter(
        lax.dot_general(grad_block, head_weight, contract, preferred_element_type=jnp.float32),
        "vocab",
        scatter_dimension=0,
        tiled=True,
    )
    hidden_grad = summed.reshape(group_count, row_count, model_width).astype(jnp.bfloat16)
    weight_grad = jnp.zeros((model_width, head_weight.shape[1]), jnp.bfloat16)
    for group_index in range(group_count):
        product_term = lax.dot_general(
            shard_rows[group_index],
            logit_grad[group_index],
            (((0,), (0,)), ((), ())),
            preferred_element_type=jnp.float32,
        )
        weight_grad = (weight_grad.astype(jnp.float32) + product_term).astype(jnp.bfloat16)
    own_loss = lax.dynamic_slice_in_dim(
        token_loss, lax.axis_index("vocab") * row_count, row_count, 1
    )
    return (own_loss, hidden_grad, weight_grad)


def subsets(masks):
    out = [0]
    for m in masks:
        out += [o ^ m for o in out]
    return out


def axis_orders(n):
    z = [1 << b for b in range(n.bit_length() - 2, 2, -1)]
    return {"zyx": z + [4, 2, 1], "xzy": [2] + z + [4, 1], "yxz": [4, 2] + z + [1]}


def kernel(n, parts, groups, hid, w_hbm, t_hbm, hfull, dl_hbm, hgrad, loss,
           hbuf, w, t, logits, dl, g, rbuf, st, stc,
           ag_send, ag_recv, rs_send, rs_recv, st_send, st_recv, local):
    bit_count = n.bit_length() - 1
    me = lax.axis_index("vocab")
    flip = [(1 - 2 * ((me // (1 << b)) % 2)) * (1 << b) for b in range(bit_count)]

    def at(mask):
        return me + sum(flip[b] for b in range(bit_count) if mask >> b & 1)

    rows, width = hid.shape
    tokens, columns = dl.shape
    part_ids = range(len(parts))
    orders = [order for _, _, order in parts]
    near = subsets([1, 2, 4])[1:]
    far = subsets([1 << b for b in range(3, bit_count)])[1:]
    peers = sorted(set(near + far + [m for order in orders for m in order]))

    copy_w = [
        pltpu.make_async_copy(w_hbm.at[pl.ds(o, c)], w.at[pl.ds(o, c)], local.at[i])
        for i, (o, c, _) in enumerate(parts)
    ]
    base = len(parts)
    copy_t = [
        pltpu.make_async_copy(t_hbm.at[c], t.at[:, c], local.at[base + 3 + c]) for c in range(groups)
    ]
    copy_own = pltpu.make_async_copy(hid, hbuf.at[me], local.at[base])
    copy_own.start()

    barrier = pltpu.get_barrier_semaphore()
    for mask in peers:
        pl.semaphore_signal(barrier, inc=1, device_id=(at(mask),), device_id_type=MESH)
    pl.semaphore_wait(barrier, len(peers))
    copy_own.wait()

    def gather_copy(p, b, r):
        o, c, _ = parts[p]
        block = hbuf.at[at(r), :, pl.ds(o, c)]
        return pltpu.make_async_remote_copy(
            src_ref=block, dst_ref=block,
            send_sem=ag_send.at[p, r ^ b], recv_sem=ag_recv.at[p, r ^ b],
            device_id=(at(b),), device_id_type=MESH)

    def gather_arrival(p, b, r):
        o, c, _ = parts[p]
        block = hbuf.at[at(r ^ b), :, pl.ds(o, c)]
        return pltpu.make_async_remote_copy(
            src_ref=block, dst_ref=block,
            send_sem=ag_send.at[p, r ^ b], recv_sem=ag_recv.at[p, r ^ b],
            device_id=(at(b),), device_id_type=MESH)

    def logits_part(p):
        o, c, _ = parts[p]
        copy_w[p].wait()

        @pl.loop(0, columns // 256)
        def _(j):
            cols = pl.ds(pl.multiple_of(j * 256, 256), 256)
            term = jnp.dot(hbuf[:, :, o:o + c].reshape(tokens, c), w[o:o + c, cols],
                           preferred_element_type=jnp.float32)
            if p == 0:
                logits[:, cols] = term
            else:
                logits[:, cols] += term

    for s in range(bit_count):
        for p in part_ids:
            gather_copy(p, orders[p][s], 0).start()
    for p in part_ids:
        copy_w[p].start()
    for copy in copy_t:
        copy.start()
    for s in range(bit_count - 1):
        for p in part_ids:
            b = orders[p][s]
            for r in subsets(orders[p][:s]):
                gather_arrival(p, b, r).wait_recv()
                for later in orders[p][s + 1:]:
                    gather_copy(p, later, r ^ b).start()
    for p in part_ids:
        for r in subsets(orders[p][:-1]):
            gather_arrival(p, orders[p][-1], r).wait_recv()
        logits_part(p)
    out_h = pltpu.make_async_copy(hbuf, hfull, local.at[base + 1])
    out_h.start()
    for copy in copy_t:
        copy.wait()

    chunk = 64
    owners = chunk // rows

    def teacher_rows(i):
        part = t[pl.ds(i * owners, owners)]
        return part.astype(jnp.float32).reshape(chunk, columns)

    @pl.loop(0, tokens // chunk)
    def _(i):
        ds = pl.ds(pl.multiple_of(i * chunk, chunk), chunk)
        l = logits[ds, :]
        tw = teacher_rows(i)
        peak = jnp.max(l, axis=-1, keepdims=True)
        total = jnp.sum(jnp.exp(l - peak), axis=-1, keepdims=True)
        mass = jnp.sum(tw, axis=-1, keepdims=True)
        cross = jnp.sum(tw * l, axis=-1, keepdims=True)
        lane = lax.broadcasted_iota(jnp.int32, (chunk, 128), 1)
        st[ds, :] = jnp.where(lane == 0, peak, jnp.where(lane == 1, total, jnp.where(lane == 2, mass, cross)))

    lines = tokens // 128
    for j in range(lines):
        turned = st[j * 128:(j + 1) * 128, :].T
        for k in range(4):
            stc[0, k, j:j + 1, :] = turned[k:k + 1]

    def exchange(source, masks):
        copies = [
            pltpu.make_async_remote_copy(
                src_ref=stc.at[source], dst_ref=stc.at[mask],
                send_sem=st_send.at[mask], recv_sem=st_recv.at[mask],
                device_id=(at(mask),), device_id_type=MESH)
            for mask in masks
        ]
        for copy in copies:
            copy.start()
        for copy in copies:
            copy.wait()
        slots = [source] + masks
        peak = functools.reduce(jnp.maximum, [stc[m, 0] for m in slots])
        total = sum(stc[m, 1] * jnp.exp(stc[m, 0] - peak) for m in slots)
        return peak, total, sum(stc[m, 2] for m in slots), sum(stc[m, 3] for m in slots)

    for k, value in enumerate(exchange(0, near)):
        stc[n, k] = value
    peak, total, mass, cross = exchange(n, far)
    log_norm = peak + jnp.log(total)
    line = lax.broadcasted_iota(jnp.int32, (128, 128), 0)
    for j in range(lines):
        st[j * 128:(j + 1) * 128, :] = jnp.where(line == 0, log_norm[j:j + 1], mass[j:j + 1]).T

    @pl.loop(0, tokens // chunk)
    def _(i):
        ds = pl.ds(pl.multiple_of(i * chunk, chunk), chunk)
        s = st[ds, :]
        dl[ds, :] = (s[:, 1:2] * jnp.exp(logits[ds, :] - s[:, 0:1]) - teacher_rows(i)).astype(jnp.bfloat16)

    out_dl = pltpu.make_async_copy(dl, dl_hbm, local.at[base + 2])
    out_dl.start()

    def scatter_copy(p, b, k):
        o, c, _ = parts[p]
        return pltpu.make_async_remote_copy(
            src_ref=g.at[at(k), :, pl.ds(o, c)], dst_ref=rbuf.at[k, :, pl.ds(o, c)],
            send_sem=rs_send.at[p, k], recv_sem=rs_recv.at[p, k],
            device_id=(at(b),), device_id_type=MESH)

    backs = [order[::-1] for order in orders]

    for p in part_ids:
        o, c, _ = parts[p]

        @pl.loop(0, c // 256)
        def _(j):
            ds = pl.ds(pl.multiple_of(o + j * 256, 256), 256)
            term = lax.dot_general(dl[...], w[ds, :], (((1,), (1,)), ((), ())),
                                   preferred_element_type=jnp.float32)
            g[:, :, ds] = term.astype(jnp.bfloat16).reshape(n, rows, 256)

        for r in subsets(backs[p][:0:-1])[::-1]:
            scatter_copy(p, backs[p][0], r ^ backs[p][0]).start()

    def reduced(p, s, k):
        o, c, _ = parts[p]
        total = g[at(k), :, o:o + c].astype(jnp.float32)
        for b in backs[p][:s]:
            scatter_copy(p, b, k ^ b).wait_recv()
            total += rbuf[k ^ b, :, o:o + c].astype(jnp.float32)
        return total.astype(jnp.bfloat16)

    for s in range(1, bit_count):
        for p in part_ids:
            o, c, _ = parts[p]
            b = backs[p][s]
            for r in subsets(backs[p][:s:-1])[::-1]:
                g[at(r ^ b), :, o:o + c] = reduced(p, s, r ^ b)
                scatter_copy(p, b, r ^ b).start()
    for p in part_ids:
        o, c, _ = parts[p]
        hgrad[:, o:o + c] = reduced(p, bit_count, 0)

    group_rows = rows // groups
    value = mass * log_norm - cross
    token = lax.broadcasted_iota(jnp.int32, value.shape, 0) * 128 + lax.broadcasted_iota(jnp.int32, value.shape, 1)
    first = me * rows
    picked = []
    for c in range(groups):
        start = first + c * group_rows
        own = jnp.where((token >= start) & (token < start + group_rows), value, 0.0)
        picked.append(jnp.sum(own, axis=0, keepdims=True))
    spread = (
        lax.broadcasted_iota(jnp.int32, (128, group_rows), 0) % group_rows
        == lax.broadcasted_iota(jnp.int32, (128, group_rows), 1)
    ).astype(jnp.float32)
    loss[...] = jnp.dot(jnp.concatenate(picked, axis=0), spread, precision=lax.Precision.HIGHEST,
                        preferred_element_type=jnp.float32)

    for p in part_ids:
        for s in range(bit_count):
            for r in subsets(orders[p][:s]):
                gather_copy(p, orders[p][s], r).wait_send()
            for r in subsets(backs[p][s + 1:]):
                scatter_copy(p, backs[p][s], r ^ backs[p][s]).wait_send()
    out_h.wait()
    out_dl.wait()


def split_width(width, orders):
    tiles = width // 256
    last = max(1, tiles // 14)
    second = max(1, tiles * 5 // 14)
    first = tiles - second - last
    half = first // 2
    sizes = [(half, "zyx"), (second, "xzy"), (first - half, "zyx"), (last, "yxz")]
    parts, at = [], 0
    for size, name in sizes:
        if size:
            parts.append((at * 256, size * 256, orders[name]))
            at += size
    return parts


def shards(n, hidden, head_weight, teacher):
    group_count, row_count, width = hidden.shape
    columns = head_weight.shape[1]
    rows = group_count * row_count
    tokens = n * rows
    bf16, f32 = jnp.bfloat16, jnp.float32
    parts = split_width(width, axis_orders(n))
    count = len(parts)
    vmem = pl.BlockSpec(memory_space=pltpu.VMEM)
    hbm = pl.BlockSpec(memory_space=pl.ANY)
    dma = pltpu.SemaphoreType.DMA
    hfull, dl, hgrad, loss = pl.pallas_call(
        functools.partial(kernel, n, parts, group_count),
        out_shape=[
            jax.ShapeDtypeStruct((n, rows, width), bf16),
            jax.ShapeDtypeStruct((tokens, columns), bf16),
            jax.ShapeDtypeStruct((rows, width), bf16),
            jax.ShapeDtypeStruct((group_count, row_count), f32),
        ],
        in_specs=[vmem, hbm, hbm],
        out_specs=[hbm, hbm, vmem, vmem],
        scratch_shapes=[
            pltpu.VMEM((n, rows, width), bf16),
            pltpu.VMEM((width, columns), bf16),
            pltpu.VMEM((n, group_count, row_count, columns), bf16),
            pltpu.VMEM((tokens, columns), f32),
            pltpu.VMEM((tokens, columns), bf16),
            pltpu.VMEM((n, rows, width), bf16),
            pltpu.VMEM((n, rows, width), bf16),
            pltpu.VMEM((tokens, 128), f32),
            pltpu.VMEM((n + 1, 4, tokens // 128, 128), f32),
            dma((count, n)), dma((count, n)), dma((count, n)), dma((count, n)),
            dma((n,)), dma((n,)), dma((count + 3 + group_count,)),
        ],
        compiler_params=pltpu.CompilerParams(
            collective_id=0, has_side_effects=True, vmem_limit_bytes=58 * 1024 * 1024),
    )(hidden.reshape(rows, width), head_weight, teacher.reshape(group_count, n, row_count, columns))
    weight_grad = lax.dot_general(
        hfull.reshape(tokens, width), dl, (((0,), (0,)), ((), ())), preferred_element_type=f32
    ).astype(bf16)
    return (loss, hgrad.reshape(group_count, row_count, width), weight_grad)


def choose(n, hidden, head_weight, teacher):
    group_count, row_count, width = hidden.shape
    fits = (
        n >= 16 and n & (n - 1) == 0 and group_count * row_count in (16, 32, 64) and row_count % 8 == 0
        and n * group_count * row_count % 128 == 0 and 128 % row_count == 0
        and width % 256 == 0 and width >= 1024 and head_weight.shape[1] % 256 == 0
    )
    if fits:
        return shards(n, hidden, head_weight, teacher)
    return plain_shards(hidden, head_weight, teacher)


def solution(mesh):
    in_specs = (P(None, "vocab", None), P(None, "vocab"), P(None, None, "vocab"))
    out_specs = (P(None, "vocab"), P(None, "vocab", None), P(None, "vocab"))
    return jax.shard_map(functools.partial(choose, mesh.shape["vocab"]), mesh=mesh, in_specs=in_specs, out_specs=out_specs, check_vma=False)
```

time: 96.7 us -> 81.4 us (0.84)
  Pallas kernels: 83.9 us -> 71.6 us
  local copies, waits for them, and re-layouts: 4.17 us -> 1.22 us
    pallas_call x1, Pallas kernels: 83.9 us -> 71.6 us  [shards(): pl.pallas_call(functools.partial(kernel, n, parts, group_count), out_shap...]
    reshape x2 -> x0, local copies, waits for them, and re-layouts: 2.71 us -> none  [the longest x1 2.07 us: shards(): teacher.reshape(group_count, n, row_count, columns).transpose(1, 0, 2, 3)]
where the time goes in v2:
time: 81.4 us; the launch traced here: 81.3 us
  Pallas kernels  71.6 us (88%)
  matrix products  7.78 us (10%)
  local copies, waits for them, and re-layouts  1.22 us (1%)
    pallas_call x1, Pallas kernels, shards(): pl.pallas_call(functools.partial(kernel, n, parts, group_count), out_shap...  71.6 us
    dot_general x1, matrix products, shards(): lax.dot_general(hfull.reshape(tokens, width), dl, (((0,), (0,)), ((), ())...  7.78 us

profile of v2, /device:TPU:0, one launch (start us, length us, event | category | flops | bytes accessed | tf_op | source)
XLA Modules:
  0.0 81.3 jit_solution(11062555567174145455)
XLA Ops:
  0.6 71.6 %shard_map.58 = (bf16[32,16,3584]{2,1,0:T(8,128)(2,1)}, bf16[512,768]{1,0:T(8,128)(2,1)}, bf16[16,3584]{1,0:T(8,128)(2,1)}, f32[2,8]{1,0:T(2,128)}) custom-call(bf16[16,3584]{1,0:T(8,128)(2,1)} %bitcast.8, bf16[3584,768]{1,0:T(8,128)(2,1)} %w_hbm.1, bf16[2,32,8,768]{3,2,1,0:T(8,128)(2,1)} %bitcast.6), custom_call_target="tpu_custom_call" | custom-call | tf_op jit(solution)/shard_map/pallas_call | solution.py:317
  72.2 0.0 copy-start.1
  72.2 0.0 copy-start
  72.3 7.8 %convolution_convert_fusion = bf16[3584,768]{1,0:T(8,128)(2,1)} fusion(bf16[512,3584]{1,0:T(8,128)(2,1)} %bitcast.9, bf16[512,768]{1,0:T(8,128)(2,1)} %get-tuple-element.10), kind=kOutput, calls=%fused_computation | convolution fusion | flops 2821324800 | bytes 9961472 | tf_op jit(solution)/shard_map/dot_general | solution.py:343
  80.0 0.0 copy-done.1
  80.0 0.6 copy.8
  80.6 0.0 copy-done
  80.6 0.6 copy.9
Async XLA Ops:
  72.2 7.8 %copy-start.1 = (f32[2,8]{1,0:T(2,128)S(1)}, f32[2,8]{1,0:T(2,128)}, u32[]{:S(2)}) copy-start(f32[2,8]{1,0:T(2,128)} %get-tuple-element.14) | copy-start | bytes 196
  72.2 8.4 %copy-start = (bf16[16,3584]{1,0:T(8,128)(2,1)S(1)}, bf16[16,3584]{1,0:T(8,128)(2,1)}, u32[]{:S(2)}) copy-start(bf16[16,3584]{1,0:T(8,128)(2,1)} %get-tuple-element.8) | copy-start | bytes 344068
